TPU v7x, 512 devices: a 8x2x16 block of a 8x8x16 slice. The times are simulated.
512 devices in a mesh: groups: 2 (over y), ctx: 16 (over z), seq: 8 (over x), head: 2 (over core).
Axes of the slice: x: 8, y: 2, z: 16, core: 2. Of those that a mesh axis runs over, the one named last changes fastest.
The devices are a block of a 8x8x16 slice.
Arguments:
- queries: bfloat16 [16, 4, 128, 576], P(('groups', 'seq'), None, ('ctx', 'head')), parts along dimension 0, may hold values from -36 to 36
- cache: bfloat16 [16, 49152, 576], P(('groups', 'seq'), 'ctx'), parts along dimension 0, may hold values from -8 to 8
- lengths: int32 [16], P(('groups', 'seq')), parts along dimension 0, may hold values from 12288 to 49152, as said below
- offsets: int32 [16, 4], P(('groups', 'seq')), parts along dimension 0, may hold values from 0 to 3
- w_uv: bfloat16 [128, 512, 128], P(('ctx', 'head')), may hold values from -0.25 to 0.25
- w_out: bfloat16 [16384, 7168], P(('ctx', 'head'), 'seq'), may hold values from -0.046875 to 0.046875
Outputs:
- mixed: bfloat16 [64, 7168], P(('groups', 'ctx', 'head'), 'seq'), parts along dimension 0
There are 2 independent parts, one for each index of `groups`. A program takes and returns all parts, laid end to end along the dimension named above; an argument that names none is the same for every part. Nothing has to cross between parts.
Inputs may be any that keep to these rules, and one draw needn't show every extreme that they name: `lengths`: each sequence's filled length, its 4 draft tokens included; some sequence reaches 49152 in every draw. Draft token t of sequence s sits at position lengths[s] - 4 + offsets[s, t].
All inputs are finite; a program needn't handle non-finite values.
Results may differ from a plain program's by a relative error of at most 0.014.
Values may be sent and summed in bfloat16 or wider, within the bound.
No kernel may reach another device: no remote copies, remote signals or barrier semaphores. Data moves between devices by JAX's collectives and lax.ppermute only.
A program may use at most 64 MiB of HBM per device.

v0:
```python
import math
import jax
import jax.numpy as jnp
from jax import lax
from jax.sharding import PartitionSpec as P

LATENT = 512
ROPE = 64
NOPE = 128
DRAFT = 4
theta = 10000.0
negative = -1e30


def copy_for_each(value, axis):
    devices = lax.axis_size(axis)
    return lax.all_to_all(
        jnp.broadcast_to(value[None], (devices, *value.shape)), axis, 0, 0, tiled=True
    )


def taken_together(value, axis):
    return copy_for_each(value, axis).max(axis=0)


def cut_along(value, dim, devices):
    dims = value.shape
    blocks = value.reshape(*dims[:dim], devices, dims[dim] // devices, *dims[dim + 1 :])
    return jnp.moveaxis(blocks, dim, 0)


def sent_and_summed(value, axis, dim):
    blocks = cut_along(value, dim, lax.axis_size(axis))
    arrived = lax.all_to_all(blocks, axis, split_axis=0, concat_axis=0, tiled=True)
    return arrived.sum(axis=0)


def sent_together(arrays, axis, dim, along):
    widths = [math.prod(a.shape[along:]) for a in arrays]
    both = jnp.concatenate(
        [a.reshape(*a.shape[:along], w) for a, w in zip(arrays, widths)], axis=along
    )
    result = sent_and_summed(both, axis, dim)
    blocks = jnp.split(result, [sum(widths[:k]) for k in range(1, len(widths))], axis=along)
    return tuple(
        (b.reshape(*result.shape[:along], *a.shape[along:]) for a, b in zip(arrays, blocks))
    )


def joined_along(blocks, dim):
    blocks = jnp.moveaxis(blocks, 0, dim)
    dims = blocks.shape
    return blocks.reshape(*dims[:dim], dims[dim] * dims[dim + 1], *dims[dim + 2 :])


def collect(value, axis, dim):
    return joined_along(copy_for_each(value, axis), dim)


def rotate(queries, positions):
    half_rope = ROPE // 2
    frequency = theta ** (-2.0 * jnp.arange(half_rope, dtype=jnp.float32) / ROPE)
    angles = positions.astype(jnp.float32)[..., None] * frequency
    cosine = jnp.cos(angles)[..., None, :]
    sine_part = jnp.sin(angles)[..., None, :]
    front_half = queries[..., LATENT : LATENT + half_rope].astype(jnp.float32)
    back_half = queries[..., LATENT + half_rope :].astype(jnp.float32)
    turned = jnp.concatenate(
        [front_half * cosine - back_half * sine_part, back_half * cosine + front_half * sine_part],
        axis=-1,
    )
    return jnp.concatenate([queries[..., :LATENT], turned.astype(jnp.bfloat16)], axis=-1)


def score_rows(blocks, limits, cache_rows, first_place):
    scores = lax.dot_general(
        blocks, cache_rows, (((1,), (1,)), ((), ())), preferred_element_type=jnp.float32
    ) * (NOPE + ROPE) ** (-0.5)
    places = first_place + jnp.arange(cache_rows.shape[0], dtype=jnp.int32)
    visible = places[None, :] <= limits[:, None]
    return (scores, visible)


def per_device(queries, cache, lengths, offsets, w_uv, w_out):
    head_count = queries.shape[2]
    entries = queries.shape[3]
    positions = lengths[0] - DRAFT + offsets[0]
    rotated = rotate(queries[0], positions)
    cache_rows = cache[0]
    values = cache_rows[:, :LATENT]
    first_place = lax.axis_index("ctx") * cache_rows.shape[0]
    devices_ctx = lax.axis_size("ctx")
    blocks = rotated.reshape(DRAFT * head_count, entries)
    gathered = lax.all_gather(blocks, "ctx", axis=0, tiled=True)
    limits = jnp.tile(jnp.repeat(positions, head_count), devices_ctx)
    scores, visible = score_rows(gathered, limits, cache_rows, first_place)
    maxima = jnp.max(jnp.where(visible, scores, negative), axis=1)
    peaks = taken_together(maxima, "ctx")
    weights = jnp.where(visible, jnp.exp(scores - peaks[:, None]), 0.0)
    totals = jnp.sum(weights, axis=1)
    numerators = jnp.dot(weights.astype(jnp.bfloat16), values, preferred_element_type=jnp.float32)
    numerators, totals = sent_together((numerators, totals), "ctx", 0, 1)
    attended = (
        (numerators / totals[:, None]).astype(jnp.bfloat16).reshape(DRAFT, head_count, LATENT)
    )
    head_values = jnp.einsum(
        "thl,hlv->thv", attended, w_uv, preferred_element_type=jnp.float32
    ).astype(jnp.bfloat16)
    head_values = head_values.reshape(DRAFT, head_count * head_values.shape[2])
    every_token = collect(head_values, "seq", 0)
    return sent_and_summed(
        jnp.dot(every_token, w_out, preferred_element_type=jnp.float32), ("ctx", "head"), 0
    ).astype(jnp.bfloat16)


def solution(mesh):
    in_specs = (
        P(("groups", "seq"), None, ("ctx", "head"), None),
        P(("groups", "seq"), "ctx", None),
        P(("groups", "seq")),
        P(("groups", "seq"), None),
        P(("ctx", "head"), None, None),
        P(("ctx", "head"), "seq"),
    )
    out_specs = P(("groups", "ctx", "head"), "seq")
    return jax.shard_map(
        per_device, mesh=mesh, in_specs=in_specs, out_specs=out_specs, check_vma=False
    )
```

profile of v0, /device:TPU:80, one launch (start us, length us, event | category | flops | bytes accessed | tf_op | source)
XLA Modules:
  0.0 169.3 jit_solution(17803864457834293212)
XLA Ops:
  0.0 0.0 copy-start
  0.7 0.7 fusion.19
  1.4 0.1 broadcast_in_dim.15
  1.5 0.1 tile.7
  1.6 0.1 le.16
  1.7 0.7 slice.16
  2.4 0.1 multiply_cosine_fusion
  2.5 0.8 fusion.14
  3.3 0.1 pad_maximum_fusion.1
  3.4 69.8 %all_gather.3 = bf16[256,576]{1,0:T(8,128)(2,1)S(1)} all-gather(bf16[16,576]{1,0:T(8,128)(2,1)S(1)} %reshape.103), channel_id=1, replica_groups=mesh['groups'=2,'ctx'=16,'seq'=8,'head'=2] {'ctx'}, dimensions={0}, use_global_device_ids=true | all-gather | bytes 313344 | tf_op jit(solution)/shard_map/all_gather | solution.py:94
  73.3 5.2 %fusion = (f32[256]{0:T(256)S(1)}, f32[256,3072]{1,0:T(8,128)}) fusion(s32[3072]{0:T(1024)S(1)} %iota_add_fusion, s32[256]{0:T(256)S(1)} %le.16, bf16[256,576]{1,0:T(8,128)(2,1)S(1)} %all_gather.3, bf16[1,3072,576]{1,2,0:T(8,128)(2,1)} %param.7), kind=kOutput, calls=%fused_computation.3 | convolution fusion | flops 909115136 | bytes 6993920 | tf_op jit(solution)/shard_map/dot_general | solution.py:76
  78.5 15.5 %all_to_all.21 = f32[16,1,256]{2,1,0:T(1,128)S(1)} all-to-all(f32[16,1,256]{2,1,0:T(1,128)S(1)} %broadcast_in_dim.31), channel_id=1, replica_groups=mesh['groups'=2,'ctx'=16,'seq'=8,'head'=2] {'ctx'}, dimensions={0} | all-to-all | bytes 32768 | tf_op jit(solution)/shard_map/all_to_all | solution.py:17
  94.0 0.0 copy-start.1
  94.0 2.8 %fusion.3 = f32[256]{0:T(256)S(1)} fusion(f32[256,3072]{1,0:T(8,128)} %get-tuple-element.12, f32[256]{0:T(256)S(1)} %reduce_max.19, s32[3072]{0:T(1024)S(1)} %iota_add_fusion, s32[256]{0:T(256)S(1)} %le.16), kind=kLoop, calls=%fused_computation.6 | loop fusion | flops 3145472 | bytes 3161088 | tf_op jit(solution)/shard_map/reduce_sum | solution.py:100
  96.8 0.0 copy-done.1
  96.8 3.0 %fusion.1 = f32[256,512]{1,0:T(8,128)S(1)} fusion(bf16[3072,576]{0,1:T(8,128)(2,1)} %bitcast.24, f32[256,3072]{1,0:T(8,128)S(1)} %copy-done.1, f32[256]{0:T(256)S(1)} %reduce_max.19, s32[3072]{0:T(1024)S(1)} %iota_add_fusion, s32[256]{0:T(256)S(1)} %le.16), kind=kOutput, calls=%fused_computation.4 | convolution fusion | flops 808452096 | bytes 6830080 | tf_op jit(solution)/shard_map/dot_general | solution.py:101
  99.8 0.0 copy-start.2
  99.8 0.2 concatenate.18
  100.0 0.1 pad_maximum_fusion
  100.1 31.9 %all_to_all.22 = f32[16,16,513]{2,1,0:T(8,128)S(1)} all-to-all(f32[16,16,513]{2,1,0:T(8,128)S(1)} %pad_maximum_fusion), channel_id=1, replica_groups=mesh['groups'=2,'ctx'=16,'seq'=8,'head'=2] {'ctx'}, dimensions={0} | all-to-all | bytes 1050624 | tf_op jit(solution)/shard_map/all_to_all | solution.py:34
  132.1 0.1 slice_reduce_fusion
  132.2 0.1 fusion.11
  132.3 0.0 copy-done.2
  132.3 0.2 fusion.10
  132.5 15.1 %all_to_all.23 = bf16[8,4,512]{2,1,0:T(4,128)(2,1)S(1)} all-to-all(bf16[8,4,512]{2,1,0:T(4,128)(2,1)S(1)} %broadcast_in_dim.34), channel_id=1, replica_groups=mesh['groups'=2,'ctx'=16,'seq'=8,'head'=2] {'seq'}, dimensions={0} | all-to-all | bytes 65536 | tf_op jit(solution)/shard_map/all_to_all | solution.py:17
  147.6 0.0 copy-done
  147.7 0.3 convolution_bitcast_fusion
  147.9 0.1 copy.21
  148.1 20.6 %all_to_all.24 = f32[32,1,896]{2,1,0:T(1,128)S(1)} all-to-all(f32[32,1,896]{2,1,0:T(1,128)S(1)} %copy.21), channel_id=1, replica_groups=mesh['groups'=2,'ctx'=16,'seq'=8,'head'=2] {'ctx','head'}, dimensions={0} | all-to-all | bytes 229376 | tf_op jit(solution)/shard_map/all_to_all | solution.py:34
  168.7 0.1 reduce_sum.29
  168.8 0.6 convert_element_type.48
  (10 shorter events, 0.2 us)
Async XLA Ops:
  0.0 147.6 %copy-start = (bf16[512,896]{1,0:T(8,128)(2,1)S(1)}, bf16[512,896]{1,0:T(8,128)(2,1)}, u32[]{:S(2)}) copy-start(bf16[512,896]{1,0:T(8,128)(2,1)} %param.11) | copy-start | bytes 2752516
  94.0 2.8 %copy-start.1 = (f32[256,3072]{1,0:T(8,128)S(1)}, f32[256,3072]{1,0:T(8,128)}, u32[]{:S(2)}) copy-start(f32[256,3072]{1,0:T(8,128)} %get-tuple-element.12) | copy-start | bytes 9437188
  99.8 32.5 %copy-start.2 = (bf16[4,512,128]{2,1,0:T(8,128)(2,1)S(1)}, bf16[4,512,128]{2,1,0:T(8,128)(2,1)}, u32[]{:S(2)}) copy-start(bf16[4,512,128]{2,1,0:T(8,128)(2,1)} %param.10) | copy-start | bytes 1572868
where the time goes:
time: 170 us; the launch traced here: 169 us
  blocking collectives  153 us (90%)
  matrix products  8.6 us (5%)
  other arithmetic  4.82 us (3%)
  local copies, waits for them, and re-layouts  2.13 us (1%)
    all_gather x1, blocking collectives, per_device(): gathered = lax.all_gather(blocks, 'ctx', axis=0, tiled=True)  69.8 us
    all_to_all x2, blocking collectives, sent_and_summed(): lax.all_to_all(blocks, axis, split_axis=0, concat_axis=0, tiled=True)  52.5 us
    all_to_all x2, blocking collectives, copy_for_each(): lax.all_to_all(jnp.broadcast_to(value[None], (devices, *value.shape)), ax...  30.6 us
    dot_general x1, matrix products, score_rows(): lax.dot_general(blocks, cache_rows, (((1,), (1,)), ((), ())), preferred_e...  5.18 us

commit v1 on v0

--- a/solution.py
+++ b/solution.py
@@ -10,6 +10,12 @@
 DRAFT = 4
 theta = 10000.0
 negative = -1e30
+
+
+def gather_by_exchange(x, axis, dim):
+    size = lax.axis_size(axis)
+    repeats = [size if d == dim else 1 for d in range(x.ndim)]
+    return lax.all_to_all(jnp.tile(x, repeats), axis, split_axis=dim, concat_axis=dim, tiled=True)
 
 
 def copy_for_each(value, axis):
@@ -91,7 +97,7 @@
     first_place = lax.axis_index("ctx") * cache_rows.shape[0]
     devices_ctx = lax.axis_size("ctx")
     blocks = rotated.reshape(DRAFT * head_count, entries)
-    gathered = lax.all_gather(blocks, "ctx", axis=0, tiled=True)
+    gathered = gather_by_exchange(blocks, "ctx", 0)
     limits = jnp.tile(jnp.repeat(positions, head_count), devices_ctx)
     scores, visible = score_rows(gathered, limits, cache_rows, first_place)
     maxima = jnp.max(jnp.where(visible, scores, negative), axis=1)

time: 170 us -> 174 us (1.024)
  blocking collectives: 153 us -> 92.5 us
  starting transfers between devices: 0 us -> 43.7 us
  waiting for transfers between devices: 0 us -> 20.5 us
    all_gather x1 -> x0, blocking collectives: 69.8 us -> none  [per_device(): gathered = lax.all_gather(blocks, 'ctx', axis=0, tiled=True)]
    all_to_all x0 -> x1, starting transfers between devices: none -> 43.7 us  [gather_by_exchange(): lax.all_to_all(jnp.tile(x, repeats), axis, split_axis=dim, concat_axis=di...]
    all_to_all x0 -> x1, waiting for transfers between devices: none -> 20.5 us  [gather_by_exchange(): lax.all_to_all(jnp.tile(x, repeats), axis, split_axis=dim, concat_axis=di...]
    all_to_all x2, blocking collectives: 52.5 us -> 59 us  [sent_and_summed(): lax.all_to_all(blocks, axis, split_axis=0, concat_axis=0, tiled=True)]
    all_to_all x2, blocking collectives: 30.6 us -> 33.5 us  [copy_for_each(): lax.all_to_all(jnp.broadcast_to(value[None], (devices, *value.shape)), ax...]
  transfers between devices with their start and end apart: 0 -> 1, of which waited for: 0 -> 1; matrix products, arithmetic and copies ran while one was open for 0% -> 0% of each run, Pallas kernels for 0% -> 0%
where the time goes in v1:
time: 174 us
  blocking collectives  92.5 us (53%)
  starting transfers between devices  43.7 us (25%)
  waiting for transfers between devices  20.5 us (12%)
  matrix products  8.65 us (5%)
  other arithmetic  4.82 us (3%)
  local copies, waits for them, and re-layouts  2.86 us (2%)
    all_to_all x2, blocking collectives, sent_and_summed(): lax.all_to_all(blocks, axis, split_axis=0, concat_axis=0, tiled=True)  59 us
    all_to_all x1, starting transfers between devices, gather_by_exchange(): lax.all_to_all(jnp.tile(x, repeats), axis, split_axis=dim, concat_axis=di...  43.7 us
    all_to_all x2, blocking collectives, copy_for_each(): lax.all_to_all(jnp.broadcast_to(value[None], (devices, *value.shape)), ax...  33.5 us
    all_to_all x1, waiting for transfers between devices, gather_by_exchange(): lax.all_to_all(jnp.tile(x, repeats), axis, split_axis=dim, concat_axis=di...  20.5 us
    dot_general x1, matrix products, score_rows(): lax.dot_general(blocks, cache_rows, (((1,), (1,)), ((), ())), preferred_e...  5.23 us
  transfers between devices with their start and end apart: 1, of which 1 were waited for; matrix products, arithmetic and copies ran while one was open for 0% of the time, Pallas kernels for 0%

profile of v1, /device:TPU:80, one launch (start us, length us, event | category | flops | bytes accessed | tf_op | source)
XLA Modules:
  0.0 173.9 jit_solution(9925113017237754606)
XLA Ops:
  0.0 0.0 copy-start
  0.7 0.7 slice.16
  1.5 0.7 fusion.19
  2.1 0.1 multiply_cosine_fusion
  2.2 0.8 fusion.14
  3.1 0.1 pad_maximum_fusion.1
  3.2 0.7 tile.18
  3.9 43.7 %all-to-all-start = ((bf16[16,16,576]{2,1,0:T(8,128)(2,1)}), bf16[16,16,576]{2,1,0:T(8,128)(2,1)S(1)}, u32[]{:S(2)}, u32[]{:S(2)}) async-start(bf16[16,16,576]{2,1,0:T(8,128)(2,1)} %tile.18), calls=%async_computation | async-start | bytes 655360 | tf_op jit(solution)/shard_map/all_to_all | solution.py:18
  47.6 0.1 broadcast_in_dim.15
  47.7 0.1 tile.15
  47.8 0.1 le.16
  47.9 20.5 %all-to-all-done = bf16[16,16,576]{2,1,0:T(8,128)(2,1)S(1)} async-done(((bf16[16,16,576]{2,1,0:T(8,128)(2,1)}), bf16[16,16,576]{2,1,0:T(8,128)(2,1)S(1)}, u32[]{:S(2)}, u32[]{:S(2)}) %all-to-all-start) | async-done | bytes 294944 | tf_op jit(solution)/shard_map/all_to_all | solution.py:18
  68.4 5.2 %fusion = (f32[256]{0:T(256)S(1)}, f32[256,3072]{1,0:T(8,128)}) fusion(s32[3072]{0:T(1024)S(1)} %iota_add_fusion, s32[256]{0:T(256)S(1)} %le.16, bf16[256,576]{1,0:T(8,128)(2,1)S(1)} %bitcast.23, bf16[1,3072,576]{1,2,0:T(8,128)(2,1)} %param.7), kind=kOutput, calls=%fused_computation.3 | convolution fusion | flops 909115136 | bytes 6993920 | tf_op jit(solution)/shard_map/dot_general | solution.py:82
  73.7 18.4 %all_to_all.30 = f32[16,1,256]{2,1,0:T(1,128)S(1)} all-to-all(f32[16,1,256]{2,1,0:T(1,128)S(1)} %broadcast_in_dim.31), channel_id=1, replica_groups=mesh['groups'=2,'ctx'=16,'seq'=8,'head'=2] {'ctx'}, dimensions={0} | all-to-all | bytes 32768 | tf_op jit(solution)/shard_map/all_to_all | solution.py:23
  92.1 2.8 %fusion.3 = f32[256]{0:T(256)S(1)} fusion(f32[256,3072]{1,0:T(8,128)} %get-tuple-element.12, f32[256]{0:T(256)S(1)} %reduce_max.19, s32[3072]{0:T(1024)S(1)} %iota_add_fusion, s32[256]{0:T(256)S(1)} %le.16), kind=kLoop, calls=%fused_computation.6 | loop fusion | flops 3145472 | bytes 3161088 | tf_op jit(solution)/shard_map/reduce_sum | solution.py:106
  94.9 0.0 copy-done.1
  94.9 3.0 %fusion.1 = f32[256,512]{1,0:T(8,128)S(1)} fusion(bf16[3072,576]{0,1:T(8,128)(2,1)} %bitcast.26, f32[256,3072]{1,0:T(8,128)S(1)} %copy-done.1, f32[256]{0:T(256)S(1)} %reduce_max.19, s32[3072]{0:T(1024)S(1)} %iota_add_fusion, s32[256]{0:T(256)S(1)} %le.16), kind=kOutput, calls=%fused_computation.4 | convolution fusion | flops 808452096 | bytes 6830080 | tf_op jit(solution)/shard_map/dot_general | solution.py:107
  97.9 0.0 copy-start.2
  97.9 0.2 concatenate.18
  98.1 0.1 pad_maximum_fusion
  98.2 38.3 %all_to_all.31 = f32[16,16,513]{2,1,0:T(8,128)S(1)} all-to-all(f32[16,16,513]{2,1,0:T(8,128)S(1)} %pad_maximum_fusion), channel_id=1, replica_groups=mesh['groups'=2,'ctx'=16,'seq'=8,'head'=2] {'ctx'}, dimensions={0} | all-to-all | bytes 1050624 | tf_op jit(solution)/shard_map/all_to_all | solution.py:40
  136.5 0.1 slice_reduce_fusion
  136.6 0.1 fusion.11
  136.7 0.0 copy-done.2
  136.8 0.2 fusion.10
  137.0 15.2 %all_to_all.32 = bf16[8,4,512]{2,1,0:T(4,128)(2,1)S(1)} all-to-all(bf16[8,4,512]{2,1,0:T(4,128)(2,1)S(1)} %broadcast_in_dim.34), channel_id=1, replica_groups=mesh['groups'=2,'ctx'=16,'seq'=8,'head'=2] {'seq'}, dimensions={0} | all-to-all | bytes 65536 | tf_op jit(solution)/shard_map/all_to_all | solution.py:23
  152.1 0.0 copy-done
  152.1 0.3 convolution_bitcast_fusion
  152.4 0.1 copy.21
  152.5 20.7 %all_to_all.33 = f32[32,1,896]{2,1,0:T(1,128)S(1)} all-to-all(f32[32,1,896]{2,1,0:T(1,128)S(1)} %copy.21), channel_id=1, replica_groups=mesh['groups'=2,'ctx'=16,'seq'=8,'head'=2] {'ctx','head'}, dimensions={0} | all-to-all | bytes 229376 | tf_op jit(solution)/shard_map/all_to_all | solution.py:40
  173.2 0.1 reduce_sum.29
  173.3 0.6 convert_element_type.48
  (11 shorter events, 0.2 us)
Async XLA Ops:
  0.0 152.1 %copy-start = (bf16[512,896]{1,0:T(8,128)(2,1)S(1)}, bf16[512,896]{1,0:T(8,128)(2,1)}, u32[]{:S(2)}) copy-start(bf16[512,896]{1,0:T(8,128)(2,1)} %param.11) | copy-start | bytes 2752516
  3.9 64.5 %all-to-all-start = ((bf16[16,16,576]{2,1,0:T(8,128)(2,1)}), bf16[16,16,576]{2,1,0:T(8,128)(2,1)S(1)}, u32[]{:S(2)}, u32[]{:S(2)}) async-start(bf16[16,16,576]{2,1,0:T(8,128)(2,1)} %tile.18), calls=%async_computation | async-start | bytes 655360 | tf_op jit(solution)/shard_map/all_to_all | solution.py:18
  92.1 2.8 %copy-start.1 = (f32[256,3072]{1,0:T(8,128)S(1)}, f32[256,3072]{1,0:T(8,128)}, u32[]{:S(2)}) copy-start(f32[256,3072]{1,0:T(8,128)} %get-tuple-element.12) | copy-start | bytes 9437188
  97.9 38.9 %copy-start.2 = (bf16[4,512,128]{2,1,0:T(8,128)(2,1)S(1)}, bf16[4,512,128]{2,1,0:T(8,128)(2,1)}, u32[]{:S(2)}) copy-start(bf16[4,512,128]{2,1,0:T(8,128)(2,1)} %param.10) | copy-start | bytes 1572868
